TPU v7x, 32 devices: a whole 2x2x4 slice. The times are simulated.
32 devices in a mesh: groups: 2 (over y), batch: 4 (over z), blk: 4 (over x, core).
Axes of the slice: x: 2, y: 2, z: 4, core: 2. Of those that a mesh axis runs over, the one named last changes fastest.
Arguments:
- queries: bfloat16 [8, 592, 1024], P(('groups', 'batch'), 'blk'), parts along dimension 0, may hold values from -12 to 12
- key_states: bfloat16 [8, 592, 1024], P(('groups', 'batch'), 'blk'), parts along dimension 0, may hold values from -6 to 6
- value_states: bfloat16 [8, 592, 1024], P(('groups', 'batch'), 'blk'), parts along dimension 0, may hold values from -6 to 6
- residual: bfloat16 [8, 592, 768], P(('groups', 'batch'), 'blk'), parts along dimension 0, may hold values from -3 to 3
- proj_weight: bfloat16 [1024, 768], P(None, 'batch'), may hold values from -0.1875 to 0.1875
- conv_weight: bfloat16 [3, 3, 768, 384], P(None, None, 'batch'), may hold values from -0.078125 to 0.078125
Outputs:
- conv_out: bfloat16 [8, 592, 384], P(('groups', 'batch'), 'blk'), parts along dimension 0
There are 2 independent parts, one for each index of `groups`. A program takes and returns all parts, laid end to end along the dimension named above; an argument that names none is the same for every part. Nothing has to cross between parts.
All inputs are finite; a program needn't handle non-finite values.
Results may differ from a plain program's by a relative error of at most 0.0085.
Values may be sent and summed in bfloat16 or wider, within the bound.
A program may use at most 64 MiB of HBM per device.

v0:
```python
import jax
import jax.numpy as jnp
from jax import lax
from jax.sharding import PartitionSpec as P

HEADS = 16
HD = 64
COLS = 74
ROWS = 2


def extended(cells, sides, width):
    for axis, dim in sides:
        count = lax.axis_size(axis)
        ends = count - 1
        head = lax.slice_in_dim(cells, 0, width, axis=dim)
        tail = lax.slice_in_dim(cells, cells.shape[dim] - width, cells.shape[dim], axis=dim)
        cells = jnp.concatenate(
            [
                lax.ppermute(tail, axis, [(i, (i + 1) % count) for i in range(ends)]),
                cells,
                lax.ppermute(head, axis, [((i + 1) % count, i) for i in range(ends)]),
            ],
            axis=dim,
        )
    return cells


def empty_state(head_count, query_rows):
    return (
        jnp.full((head_count, query_rows), -1e30, jnp.float32),
        jnp.zeros((head_count, query_rows), jnp.float32),
        jnp.zeros((head_count, query_rows, HD), jnp.float32),
    )


def absorb(carry_state, query_block, key_block, value_block):
    row_max, weight_sum, running = carry_state
    scores = jnp.einsum(
        "qhd,khd->hqk", query_block, key_block, preferred_element_type=jnp.float32
    ) * HD ** (-0.5)
    new_max = jnp.maximum(row_max, jnp.max(scores, axis=2))
    factor = jnp.exp(row_max - new_max)
    weights = jnp.exp(scores - new_max[:, :, None])
    weight_sum = weight_sum * factor + jnp.sum(weights, axis=2)
    running = running * factor[:, :, None] + jnp.einsum(
        "hqk,khd->hqd",
        weights.astype(jnp.bfloat16),
        value_block,
        preferred_element_type=jnp.float32,
    )
    return (new_max, weight_sum, running)


def finish(carry_state):
    row_max, weight_sum, running = carry_state
    mixed = running / weight_sum[:, :, None]
    head_count, query_rows = weight_sum.shape
    return mixed.transpose(1, 0, 2).reshape(query_rows, head_count * HD).astype(jnp.bfloat16)


def body(queries, key_states, value_states, residual, proj_weight, conv_weight):
    query_rows = queries[0]
    key_rows = key_states[0]
    value_rows = value_states[0]
    tok_rows = query_rows.shape[0]
    cycle_count = lax.axis_size("blk")
    local_heads = HEADS // cycle_count
    query_all, key_all, value_all = (
        lax.all_to_all(query_rows, "blk", split_axis=1, concat_axis=0, tiled=True),
        lax.all_to_all(key_rows, "blk", split_axis=1, concat_axis=0, tiled=True),
        lax.all_to_all(value_rows, "blk", split_axis=1, concat_axis=0, tiled=True),
    )
    seq_rows = tok_rows * cycle_count
    group = 1
    while cycle_count % (group * 2) == 0 and tok_rows * group * 2 <= 1024:
        group = group * 2
    block_rows = tok_rows * group
    block_count = seq_rows // block_rows
    query_blocks = query_all.reshape(block_count, block_rows, local_heads, HD)
    key_blocks = key_all.reshape(block_count, block_rows, local_heads, HD)
    value_blocks = value_all.reshape(block_count, block_rows, local_heads, HD)

    def one_block(query_block):

        def absorb_one(index, inner_state):
            return absorb(inner_state, query_block, key_blocks[index], value_blocks[index])

        return finish(
            lax.fori_loop(0, block_count, absorb_one, empty_state(local_heads, block_rows))
        )

    mixed_rows = lax.map(one_block, query_blocks).reshape(seq_rows, local_heads * HD)
    attention = lax.all_to_all(mixed_rows, "blk", split_axis=0, concat_axis=1, tiled=True)
    projected = jnp.dot(
        attention,
        lax.all_gather(proj_weight, "batch", axis=1, tiled=True),
        preferred_element_type=jnp.float32,
    )
    hidden = (residual[0].astype(jnp.float32) + projected).astype(jnp.bfloat16)
    feature_grid = hidden.reshape(ROWS, COLS, hidden.shape[1])
    rimmed = extended(feature_grid, (("blk", 0),), 1)
    padded = jnp.pad(rimmed, ((0, 0), (1, 1), (0, 0)))
    shard_piece = lax.all_gather(conv_weight, "batch", axis=2, tiled=True)
    piece_rows = shard_piece.shape[2]
    windows = []
    for row_off in range(3):
        for col_off in range(3):
            windows.append(
                padded[row_off : row_off + ROWS, col_off : col_off + COLS].reshape(
                    tok_rows, piece_rows
                )
            )
    stacked = jnp.concatenate(windows, axis=1)
    flat_weight = shard_piece.reshape(9 * piece_rows, shard_piece.shape[3])
    conv_sum = jnp.dot(stacked, flat_weight, preferred_element_type=jnp.float32)
    return conv_sum.astype(jnp.bfloat16)[None]


def solution(mesh):
    return jax.shard_map(
        body,
        mesh=mesh,
        in_specs=(
            P(("groups", "batch"), "blk", None),
            P(("groups", "batch"), "blk", None),
            P(("groups", "batch"), "blk", None),
            P(("groups", "batch"), "blk", None),
            P(None, "batch"),
            P(None, None, "batch", None),
        ),
        out_specs=P(("groups", "batch"), "blk", None),
        check_vma=False,
    )
```

profile of v0, /device:TPU:0, one launch (start us, length us, event | category | flops | bytes accessed | tf_op | source)
XLA Modules:
  0.0 159.6 jit_solution(15283503268794246920)
XLA Ops:
  8.0 1.2 all_to_all.48
  9.9 4.2 %all-to-all-start = ((bf16[148,4,256]{2,0,1:T(8,128)(2,1)}), bf16[148,4,256]{2,0,1:T(8,128)(2,1)S(1)}, u32[]{:S(2)}, u32[]{:S(2)}) async-start(bf16[148,4,256]{2,0,1:T(8,128)(2,1)} %copy.22), calls=%async_computation | async-start | bytes 622592 | tf_op jit(solution)/shard_map/all_to_all | solution.py:70
  14.3 0.8 copy.24
  15.1 5.6 %all-to-all-done = bf16[148,4,256]{2,0,1:T(8,128)(2,1)S(1)} async-done(((bf16[148,4,256]{2,0,1:T(8,128)(2,1)}), bf16[148,4,256]{2,0,1:T(8,128)(2,1)S(1)}, u32[]{:S(2)}, u32[]{:S(2)}) %all-to-all-start) | async-done | bytes 303136 | tf_op jit(solution)/shard_map/all_to_all | solution.py:70
  20.7 3.5 %all-to-all-start.1 = ((bf16[148,4,256]{2,0,1:T(8,128)(2,1)}), bf16[148,4,256]{2,0,1:T(8,128)(2,1)S(1)}, u32[]{:S(2)}, u32[]{:S(2)}) async-start(bf16[148,4,256]{2,0,1:T(8,128)(2,1)} %copy.24), calls=%async_computation.1 | async-start | bytes 622592 | tf_op jit(solution)/shard_map/all_to_all | solution.py:71
  25.0 5.6 %all-to-all-done.1 = bf16[148,4,256]{2,0,1:T(8,128)(2,1)S(1)} async-done(((bf16[148,4,256]{2,0,1:T(8,128)(2,1)}), bf16[148,4,256]{2,0,1:T(8,128)(2,1)S(1)}, u32[]{:S(2)}, u32[]{:S(2)}) %all-to-all-start.1) | async-done | bytes 303136 | tf_op jit(solution)/shard_map/all_to_all | solution.py:71
  30.6 3.5 %all-to-all-start.2 = ((bf16[148,4,256]{2,0,1:T(8,128)(2,1)}), bf16[148,4,256]{2,0,1:T(8,128)(2,1)S(1)}, u32[]{:S(2)}, u32[]{:S(2)}) async-start(bf16[148,4,256]{2,0,1:T(8,128)(2,1)} %copy.26), calls=%async_computation.2 | async-start | bytes 622592 | tf_op jit(solution)/shard_map/all_to_all | solution.py:72
  34.7 5.9 %all-to-all-done.2 = bf16[148,4,256]{2,0,1:T(8,128)(2,1)S(1)} async-done(((bf16[148,4,256]{2,0,1:T(8,128)(2,1)}), bf16[148,4,256]{2,0,1:T(8,128)(2,1)S(1)}, u32[]{:S(2)}, u32[]{:S(2)}) %all-to-all-start.2) | async-done | bytes 303136 | tf_op jit(solution)/shard_map/all_to_all | solution.py:72
  40.9 1.1 multiply_reduce_fusion
  42.0 1.0 fusion
  43.1 1.3 fusion.17
  45.1 8.9 %all_to_all.64 = bf16[4,148,256]{2,1,0:T(8,128)(2,1)S(1)} all-to-all(bf16[4,148,256]{2,1,0:T(8,128)(2,1)S(1)} %copy.29), channel_id=1, replica_groups=mesh['groups'=2,'batch'=4,'blk'=4] {'blk'}, dimensions={0} | all-to-all | bytes 606208 | tf_op jit(solution)/shard_map/all_to_all | solution.py:94
  54.3 2.2 %fusion.12 = bf16[148,768]{1,0:T(8,128)(2,1)S(1)} fusion(bf16[148,1024]{1,0:T(8,128)(2,1)S(1)} %bitcast.41, bf16[1024,768]{0,1:T(8,128)(2,1)} %all-gather.3.cloned.1.call-done, bf16[1,148,768]{2,1,0:T(8,128)(2,1)S(1)} %copy-done.2), kind=kOutput, calls=%fused_computation.12 | convolution fusion | flops 233124864 | bytes 2330624 | tf_op jit(solution)/shard_map/dot_general | solution.py:95
  56.5 1.7 %collective-permute-start = (bf16[1,74,768]{2,1,0:T(8,128)(2,1)S(1)}, bf16[1,74,768]{2,1,0:T(8,128)(2,1)S(1)}, u32[]{:S(2)}, u32[]{:S(2)}) collective-permute-start(bf16[1,74,768]{2,1,0:T(8,128)(2,1)S(1)} %get-tuple-element.60), channel_id=1, source_target_pairs={{0,1},{1,2},{2,3},{4,5},{5,6},{6,7},{8,9},{9,10},{10,11},{12,13},{... | collective-permute-start | bytes 341000 | tf_op jit(solution)/shard_map/ppermute | solution.py:20
  58.2 1.3 collective-permute-start.1
  59.6 2.0 %collective-permute-done.1 = bf16[1,74,768]{2,1,0:T(8,128)(2,1)S(1)} collective-permute-done((bf16[1,74,768]{2,1,0:T(8,128)(2,1)S(1)}, bf16[1,74,768]{2,1,0:T(8,128)(2,1)S(1)}, u32[]{:S(2)}, u32[]{:S(2)}) %collective-permute-start.1) | collective-permute-done | bytes 113696 | tf_op jit(solution)/shard_map/ppermute | solution.py:22
  62.0 0.8 reshape.82
  62.8 0.8 reshape.83
  63.5 0.8 reshape.84
  64.5 1.0 constant_dynamic-update-slice_fusion.7
  65.5 1.0 constant_dynamic-update-slice_fusion.6
  66.5 1.0 constant_dynamic-update-slice_fusion.5
  67.5 80.7 %all-gather.5.cloned.1.call-done = bf16[3,3,768,384]{3,2,1,0:T(8,128)(2,1)} async-done(((bf16[3,3,192,384]{3,2,1,0:T(8,128)(2,1)}), bf16[3,3,768,384]{3,2,1,0:T(8,128)(2,1)}) %all-gather.5.cloned.1.call-update) | async-done | bytes 5308432 | tf_op jit(solution)/shard_map/all_gather | solution.py:104
  148.3 4.5 %fusion.13 = bf16[1,148,384]{2,1,0:T(8,128)(2,1)} fusion(bf16[148,6912]{1,0:T(8,128)(2,1)S(1)} %constant_dynamic-update-slice_fusion, bf16[6912,384]{1,0:T(8,128)(2,1)} %bitcast.37), kind=kOutput, calls=%fused_computation.14 | convolution fusion | flops 785702400 | bytes 7468032 | tf_op jit(solution)/shard_map/dot_general | solution.py:116
  (42 shorter events, 5.8 us)
Async XLA Ops:
  6.5 7.6 %copy-start = (bf16[1,148,1024]{2,1,0:T(8,128)(2,1)S(1)}, bf16[1,148,1024]{2,1,0:T(8,128)(2,1)}, u32[]{:S(2)}) copy-start(bf16[1,148,1024]{2,1,0:T(8,128)(2,1)} %param.7) | copy-start | bytes 909316
  6.5 47.8 %all-gather.3.cloned.1.call-start = ((), (), s32[]{:S(2)}) async-start(), calls=%async_computation.4 | async-start | bytes 1966080 | tf_op jit(solution)/shard_map/all_gather | solution.py:97
  7.3 141.0 %all-gather.5.cloned.1.call-start = ((), (), s32[]{:S(2)}) async-start(), calls=%async_computation.5 | async-start | bytes 6635520 | tf_op jit(solution)/shard_map/all_gather | solution.py:104
  8.0 16.1 %copy-start.1 = (bf16[1,148,1024]{2,1,0:T(8,128)(2,1)S(1)}, bf16[1,148,1024]{2,1,0:T(8,128)(2,1)}, u32[]{:S(2)}) copy-start(bf16[1,148,1024]{2,1,0:T(8,128)(2,1)} %param.8) | copy-start | bytes 909316
  9.9 10.8 %all-to-all-start = ((bf16[148,4,256]{2,0,1:T(8,128)(2,1)}), bf16[148,4,256]{2,0,1:T(8,128)(2,1)S(1)}, u32[]{:S(2)}, u32[]{:S(2)}) async-start(bf16[148,4,256]{2,0,1:T(8,128)(2,1)} %copy.22), calls=%async_computation | async-start | bytes 622592 | tf_op jit(solution)/shard_map/all_to_all | solution.py:70
  20.7 10.0 %all-to-all-start.1 = ((bf16[148,4,256]{2,0,1:T(8,128)(2,1)}), bf16[148,4,256]{2,0,1:T(8,128)(2,1)S(1)}, u32[]{:S(2)}, u32[]{:S(2)}) async-start(bf16[148,4,256]{2,0,1:T(8,128)(2,1)} %copy.24), calls=%async_computation.1 | async-start | bytes 622592 | tf_op jit(solution)/shard_map/all_to_all | solution.py:71
  30.6 10.0 %all-to-all-start.2 = ((bf16[148,4,256]{2,0,1:T(8,128)(2,1)}), bf16[148,4,256]{2,0,1:T(8,128)(2,1)S(1)}, u32[]{:S(2)}, u32[]{:S(2)}) async-start(bf16[148,4,256]{2,0,1:T(8,128)(2,1)} %copy.26), calls=%async_computation.2 | async-start | bytes 622592 | tf_op jit(solution)/shard_map/all_to_all | solution.py:72
  44.4 9.9 %copy-start.2 = (bf16[1,148,768]{2,1,0:T(8,128)(2,1)S(1)}, bf16[1,148,768]{2,1,0:T(8,128)(2,1)}, u32[]{:S(2)}) copy-start(bf16[1,148,768]{2,1,0:T(8,128)(2,1)} %param.9) | copy-start | bytes 681988
  56.5 3.0 %collective-permute-start = (bf16[1,74,768]{2,1,0:T(8,128)(2,1)S(1)}, bf16[1,74,768]{2,1,0:T(8,128)(2,1)S(1)}, u32[]{:S(2)}, u32[]{:S(2)}) collective-permute-start(bf16[1,74,768]{2,1,0:T(8,128)(2,1)S(1)} %get-tuple-element.60), channel_id=1, source_target_pairs={{0,1},{1,2},{2,3},{4,5},{5,6},{6,7},{8,9},{9,10},{10,11},{12,13},{... | collective-permute-start | bytes 341000 | tf_op jit(solution)/shard_map/ppermute | solution.py:20
  58.2 3.4 %collective-permute-start.1 = (bf16[1,74,768]{2,1,0:T(8,128)(2,1)S(1)}, bf16[1,74,768]{2,1,0:T(8,128)(2,1)S(1)}, u32[]{:S(2)}, u32[]{:S(2)}) collective-permute-start(bf16[1,74,768]{2,1,0:T(8,128)(2,1)S(1)} %get-tuple-element.61), channel_id=1, source_target_pairs={{1,0},{2,1},{3,2},{5,4},{6,5},{7,6},{9,8},{10,9},{11,10},{13,12},{... | collective-permute-start | bytes 341000 | tf_op jit(solution)/shard_map/ppermute | solution.py:22
Sparse Core Ops, SparseCore 0:
  8.9 39.7 all-gather.2
  50.2 97.9 all-gather.4
where the time goes:
time: 160 us
  waiting for transfers between devices  101 us (63%)
  starting transfers between devices  14.1 us (9%)
  between operations  13.7 us (9%)
  local copies, waits for them, and re-layouts  11.2 us (7%)
  matrix products  9.04 us (6%)
  blocking collectives  8.9 us (6%)
    all_gather x1, waiting for transfers between devices, body(): shard_piece = lax.all_gather(conv_weight, 'batch', axis=2, tiled=True)  80.7 us
    all_to_all x1, blocking collectives, body(): lax.all_to_all(mixed_rows, 'blk', split_axis=0, concat_axis=1, tiled=True)  8.9 us
    all_to_all x1, waiting for transfers between devices, body(): lax.all_to_all(value_rows, 'blk', split_axis=1, concat_axis=0, tiled=True)  5.92 us
    all_to_all x1, waiting for transfers between devices, body(): lax.all_to_all(query_rows, 'blk', split_axis=1, concat_axis=0, tiled=True)  5.62 us
    all_to_all x1, waiting for transfers between devices, body(): lax.all_to_all(key_rows, 'blk', split_axis=1, concat_axis=0, tiled=True)  5.6 us
    dot_general x1, matrix products, body(): conv_sum = jnp.dot(stacked, flat_weight, preferred_element_type=jnp.float32)  4.48 us
    all_to_all x1, starting transfers between devices, body(): lax.all_to_all(query_rows, 'blk', split_axis=1, concat_axis=0, tiled=True)  4.24 us
    all_to_all x1, starting transfers between devices, body(): lax.all_to_all(value_rows, 'blk', split_axis=1, concat_axis=0, tiled=True)  3.45 us
  transfers between devices with their start and end apart: 7, of which 5 were waited for; matrix products, arithmetic and copies ran while one was open for 10% of the time, Pallas kernels for 0%

commit v1 on v0

--- a/solution.py
+++ b/solution.py
@@ -101,7 +101,14 @@
     feature_grid = hidden.reshape(ROWS, COLS, hidden.shape[1])
     rimmed = extended(feature_grid, (("blk", 0),), 1)
     padded = jnp.pad(rimmed, ((0, 0), (1, 1), (0, 0)))
-    shard_piece = lax.all_gather(conv_weight, "batch", axis=2, tiled=True)
+    ring = [conv_weight]
+    for hop in range(3):
+        ring.append(lax.ppermute(ring[-1], "batch", [(dev, (dev + 1) % 4) for dev in range(4)]))
+    shard_piece = jnp.roll(
+        jnp.concatenate(ring[::-1], axis=2),
+        (lax.axis_index("batch") + 1) * ring[0].shape[2],
+        axis=2,
+    )
     piece_rows = shard_piece.shape[2]
     windows = []
     for row_off in range(3):

time: 160 us -> 177 us (1.11)
  local copies, waits for them, and re-layouts: 11.2 us -> 39.2 us
  waiting for transfers between devices: 101 us -> 85.3 us
  starting transfers between devices: 14.1 us -> 18.4 us
    all_gather x1 -> x0, waiting for transfers between devices: 80.7 us -> none  [body(): shard_piece = lax.all_gather(conv_weight, 'batch', axis=2, tiled=True)]
    ppermute x0 -> x3, waiting for transfers between devices: none -> 73.3 us  [body(): lax.ppermute(ring[-1], 'batch', [(dev, (dev + 1) % 4) for dev in range(4)])]
    unnamed x16 -> x33, local copies, waits for them, and re-layouts: 3.14 us -> 12.8 us
    reshape x8, local copies, waits for them, and re-layouts: 2.53 us -> 11.8 us  [body(): padded[row_off:row_off + ROWS, col_off:col_off + COLS]]
    all_to_all x1, waiting for transfers between devices: 5.92 us -> 0.86 us  [body(): lax.all_to_all(value_rows, 'blk', split_axis=1, concat_axis=0, tiled=True)]
    dot_general x1, matrix products: 4.48 us -> 2.01 us  [body(): conv_sum = jnp.dot(stacked, flat_weight, preferred_element_type=jnp.float32)]
    ppermute x0 -> x3, starting transfers between devices: none -> 2.3 us  [body(): lax.ppermute(ring[-1], 'batch', [(dev, (dev + 1) % 4) for dev in range(4)])]
    ppermute x1, waiting for transfers between devices: 2.01 us -> 0.01 us  [extended(): lax.ppermute(head, axis, [((i + 1) % count, i) for i in range(ends)])]
  transfers between devices with their start and end apart: 7 -> 9, of which waited for: 5 -> 7; matrix products, arithmetic and copies ran while one was open for 10% -> 20% of each run, Pallas kernels for 0% -> 0%
where the time goes in v1:
time: 177 us; the launch traced here: 176 us
  waiting for transfers between devices  85.3 us (48%)
  local copies, waits for them, and re-layouts  39.2 us (22%)
  starting transfers between devices  18.4 us (10%)
  between operations  13.7 us (8%)
  blocking collectives  9.11 us (5%)
  matrix products  7.56 us (4%)
  other arithmetic  2.97 us (2%)
    ppermute x3, waiting for transfers between devices, body(): lax.ppermute(ring[-1], 'batch', [(dev, (dev + 1) % 4) for dev in range(4)])  73.3 us
    unnamed x33, local copies, waits for them, and re-layouts  12.8 us
    reshape x8, local copies, waits for them, and re-layouts, body(): padded[row_off:row_off + ROWS, col_off:col_off + COLS]  11.8 us
    all_to_all x1, blocking collectives, body(): lax.all_to_all(mixed_rows, 'blk', split_axis=0, concat_axis=1, tiled=True)  9.11 us
    all_to_all x1, waiting for transfers between devices, body(): lax.all_to_all(query_rows, 'blk', split_axis=1, concat_axis=0, tiled=True)  4.86 us
    all_to_all x1, waiting for transfers between devices, body(): lax.all_to_all(key_rows, 'blk', split_axis=1, concat_axis=0, tiled=True)  4.65 us
    all_to_all x1, starting transfers between devices, body(): lax.all_to_all(key_rows, 'blk', split_axis=1, concat_axis=0, tiled=True)  4.24 us
    all_to_all x1, starting transfers between devices, body(): lax.all_to_all(value_rows, 'blk', split_axis=1, concat_axis=0, tiled=True)  4.09 us
  transfers between devices with their start and end apart: 9, of which 7 were waited for; matrix products, arithmetic and copies ran while one was open for 20% of the time, Pallas kernels for 0%

profile of v1, /device:TPU:0, one launch (start us, length us, event | category | flops | bytes accessed | tf_op | source)
XLA Modules:
  0.0 176.3 jit_solution(636547361825307031)
XLA Ops:
  8.5 4.2 %all-to-all-start.1 = ((bf16[148,4,256]{2,0,1:T(8,128)(2,1)}), bf16[148,4,256]{2,0,1:T(8,128)(2,1)S(1)}, u32[]{:S(2)}, u32[]{:S(2)}) async-start(bf16[148,4,256]{2,0,1:T(8,128)(2,1)} %copy.24), calls=%async_computation.1 | async-start | bytes 622592 | tf_op jit(solution)/shard_map/all_to_all | solution.py:71
  14.7 4.6 %all-to-all-done.1 = bf16[148,4,256]{2,0,1:T(8,128)(2,1)S(1)} async-done(((bf16[148,4,256]{2,0,1:T(8,128)(2,1)}), bf16[148,4,256]{2,0,1:T(8,128)(2,1)S(1)}, u32[]{:S(2)}, u32[]{:S(2)}) %all-to-all-start.1) | async-done | bytes 303136 | tf_op jit(solution)/shard_map/all_to_all | solution.py:71
  19.3 3.5 %all-to-all-start = ((bf16[148,4,256]{2,0,1:T(8,128)(2,1)}), bf16[148,4,256]{2,0,1:T(8,128)(2,1)S(1)}, u32[]{:S(2)}, u32[]{:S(2)}) async-start(bf16[148,4,256]{2,0,1:T(8,128)(2,1)} %copy.22), calls=%async_computation | async-start | bytes 622592 | tf_op jit(solution)/shard_map/all_to_all | solution.py:70
  24.4 4.9 %all-to-all-done = bf16[148,4,256]{2,0,1:T(8,128)(2,1)S(1)} async-done(((bf16[148,4,256]{2,0,1:T(8,128)(2,1)}), bf16[148,4,256]{2,0,1:T(8,128)(2,1)S(1)}, u32[]{:S(2)}, u32[]{:S(2)}) %all-to-all-start) | async-done | bytes 303136 | tf_op jit(solution)/shard_map/all_to_all | solution.py:70
  30.0 4.1 %all-to-all-start.2 = ((bf16[148,4,256]{2,0,1:T(8,128)(2,1)}), bf16[148,4,256]{2,0,1:T(8,128)(2,1)}, u32[]{:S(2)}, u32[]{:S(2)}) async-start(bf16[148,4,256]{2,0,1:T(8,128)(2,1)} %copy.26), calls=%async_computation.2 | async-start | bytes 622592 | tf_op jit(solution)/shard_map/all_to_all | solution.py:72
  34.1 2.3 %collective-permute-start.2 = (bf16[3,3,192,384]{3,2,1,0:T(8,128)(2,1)S(1)}, bf16[3,3,192,384]{3,2,1,0:T(8,128)(2,1)S(1)}, u32[]{:S(2)}, u32[]{:S(2)}) collective-permute-start(bf16[3,3,192,384]{3,2,1,0:T(8,128)(2,1)S(1)} %copy-done), channel_id=1, source_target_pairs={{0,4},{4,8},{8,12},{12,0},{1,5},{5,9},{9,13},{13,1},{2,6},{6,10},{... | collective-permute-start | bytes 3981320 | tf_op jit(solution)/shard_map/ppermute | solution.py:106
  37.7 2.1 %reshape.91 = bf16[592,4,64]{2,1,0:T(4,128)(2,1)} reshape(bf16[4,148,256]{2,1,0:T(8,128)(2,1)} %bitcast.39) | data formatting | bytes 606208 | tf_op jit(solution)/shard_map/while/body/jit(dynamic_index_in_dim)/squeeze | solution.py:93
  40.7 2.1 %reshape.93 = bf16[592,4,64]{2,1,0:T(4,128)(2,1)} reshape(bf16[4,148,256]{2,1,0:T(8,128)(2,1)} %bitcast.4) | data formatting | bytes 606208 | tf_op jit(solution)/shard_map/while/body/eval_jaxpr/while/body/eval_jaxpr/squeeze | solution.py:87
  42.8 2.2 %multiply_reduce_fusion = (f32[4,592]{1,0:T(4,128)S(1)}, f32[4,592,592]{1,2,0:T(8,128)S(1)}) fusion(bf16[592,4,64]{2,1,0:T(4,128)(2,1)S(1)} %reshape.92, bf16[592,4,64]{2,1,0:T(4,128)(2,1)} %reshape.91), kind=kOutput, calls=%fused_computation.1 | convolution fusion | flops 182238912 | bytes 6223104 | tf_op jit(solution)/shard_map/while/body/eval_jaxpr/while/body/eval_jaxpr/qhd,khd->hqk/dot_general | solution.py:39
  46.1 47.3 %collective-permute-done.2 = bf16[3,3,192,384]{3,2,1,0:T(8,128)(2,1)S(1)} collective-permute-done((bf16[3,3,192,384]{3,2,1,0:T(8,128)(2,1)S(1)}, bf16[3,3,192,384]{3,2,1,0:T(8,128)(2,1)S(1)}, u32[]{:S(2)}, u32[]{:S(2)}) %collective-permute-start.2) | collective-permute-done | bytes 1327136 | tf_op jit(solution)/shard_map/ppermute | solution.py:106
  95.4 9.1 %all_to_all.64 = bf16[4,148,256]{2,1,0:T(8,128)(2,1)S(1)} all-to-all(bf16[4,148,256]{2,1,0:T(8,128)(2,1)S(1)} %copy.29), channel_id=1, replica_groups=mesh['groups'=2,'batch'=4,'blk'=4] {'blk'}, dimensions={0} | all-to-all | bytes 606208 | tf_op jit(solution)/shard_map/all_to_all | solution.py:94
  104.8 2.1 %fusion.12 = bf16[148,768]{1,0:T(8,128)(2,1)S(1)} fusion(bf16[148,1024]{1,0:T(8,128)(2,1)S(1)} %bitcast.40, bf16[1024,768]{0,1:T(8,128)(2,1)} %all-gather.2.cloned.1.call-done, bf16[1,148,768]{2,1,0:T(8,128)(2,1)} %param.9), kind=kOutput, calls=%fused_computation.12 | convolution fusion | flops 233124864 | bytes 2330624 | tf_op jit(solution)/shard_map/dot_general | solution.py:95
  108.9 3.0 %collective-permute-start = (bf16[1,74,768]{2,1,0:T(8,128)(2,1)S(1)}, bf16[1,74,768]{2,1,0:T(8,128)(2,1)S(1)}, u32[]{:S(2)}, u32[]{:S(2)}) collective-permute-start(bf16[1,74,768]{2,1,0:T(8,128)(2,1)S(1)} %get-tuple-element.60), channel_id=1, source_target_pairs={{0,1},{1,2},{2,3},{4,5},{5,6},{6,7},{8,9},{9,10},{10,11},{12,13},{... | collective-permute-start | bytes 341000 | tf_op jit(solution)/shard_map/ppermute | solution.py:20
  113.0 13.4 %collective-permute-done.3 = bf16[3,3,192,384]{3,2,1,0:T(8,128)(2,1)} collective-permute-done((bf16[3,3,192,384]{3,2,1,0:T(8,128)(2,1)S(1)}, bf16[3,3,192,384]{3,2,1,0:T(8,128)(2,1)}, u32[]{:S(2)}, u32[]{:S(2)}) %collective-permute-start.3) | collective-permute-done | bytes 1327136 | tf_op jit(solution)/shard_map/ppermute | solution.py:106
  127.5 1.7 reshape.81
  129.2 1.8 pad_maximum_fusion
  131.0 1.7 reshape.82
  132.7 1.7 reshape.83
  134.3 1.7 reshape.84
  136.0 1.7 reshape.85
  138.7 1.7 reshape.87
  146.1 12.6 %collective-permute-done.4 = bf16[3,3,192,384]{3,2,1,0:T(8,128)(2,1)} collective-permute-done((bf16[3,3,192,384]{3,2,1,0:T(8,128)(2,1)}, bf16[3,3,192,384]{3,2,1,0:T(8,128)(2,1)}, u32[]{:S(2)}, u32[]{:S(2)}) %collective-permute-start.4) | collective-permute-done | bytes 1327136 | tf_op jit(solution)/shard_map/ppermute | solution.py:106
  162.4 1.6 constant_dynamic-update-slice_fusion.12
  167.4 2.0 %fusion.13 = bf16[1,148,384]{2,1,0:T(8,128)(2,1)} fusion(bf16[148,6912]{1,0:T(8,128)(2,1)S(1)} %constant_dynamic-update-slice_fusion, bf16[6912,384]{1,0:T(8,128)(2,1)S(1)} %bitcast.37), kind=kOutput, calls=%fused_computation.14 | convolution fusion | flops 785702400 | bytes 7468032 | tf_op jit(solution)/shard_map/dot_general | solution.py:123
  (64 shorter events, 29.5 us)
Async XLA Ops:
  6.5 17.0 %copy-start.7 = (bf16[1,148,1024]{2,1,0:T(8,128)(2,1)S(1)}, bf16[1,148,1024]{2,1,0:T(8,128)(2,1)}, u32[]{:S(2)}) copy-start(bf16[1,148,1024]{2,1,0:T(8,128)(2,1)} %param.8) | copy-start | bytes 909316
  6.5 27.5 %copy-start = (bf16[3,3,192,384]{3,2,1,0:T(8,128)(2,1)S(1)}, bf16[3,3,192,384]{3,2,1,0:T(8,128)(2,1)}, u32[]{:S(2)}) copy-start(bf16[3,3,192,384]{3,2,1,0:T(8,128)(2,1)} %param.11) | copy-start | bytes 3981316
  8.5 10.8 %all-to-all-start.1 = ((bf16[148,4,256]{2,0,1:T(8,128)(2,1)}), bf16[148,4,256]{2,0,1:T(8,128)(2,1)S(1)}, u32[]{:S(2)}, u32[]{:S(2)}) async-start(bf16[148,4,256]{2,0,1:T(8,128)(2,1)} %copy.24), calls=%async_computation.1 | async-start | bytes 622592 | tf_op jit(solution)/shard_map/all_to_all | solution.py:71
  19.3 17.1 %copy-start.1 = (bf16[148,4,256]{2,0,1:T(8,128)(2,1)}, bf16[148,4,256]{2,0,1:T(8,128)(2,1)S(1)}, u32[]{:S(2)}) copy-start(bf16[148,4,256]{2,0,1:T(8,128)(2,1)S(1)} %all-to-all-done.1) | copy-start | bytes 909316
  19.3 10.0 %all-to-all-start = ((bf16[148,4,256]{2,0,1:T(8,128)(2,1)}), bf16[148,4,256]{2,0,1:T(8,128)(2,1)S(1)}, u32[]{:S(2)}, u32[]{:S(2)}) async-start(bf16[148,4,256]{2,0,1:T(8,128)(2,1)} %copy.22), calls=%async_computation | async-start | bytes 622592 | tf_op jit(solution)/shard_map/all_to_all | solution.py:70
  22.8 82.1 %all-gather.2.cloned.1.call-start = ((), (), s32[]{:S(2)}) async-start(), calls=%async_computation.4 | async-start | bytes 1966080 | tf_op jit(solution)/shard_map/all_gather | solution.py:97
  29.3 0.7 copy-start.2
  30.0 10.7 %all-to-all-start.2 = ((bf16[148,4,256]{2,0,1:T(8,128)(2,1)}), bf16[148,4,256]{2,0,1:T(8,128)(2,1)}, u32[]{:S(2)}, u32[]{:S(2)}) async-start(bf16[148,4,256]{2,0,1:T(8,128)(2,1)} %copy.26), calls=%async_computation.2 | async-start | bytes 622592 | tf_op jit(solution)/shard_map/all_to_all | solution.py:72
  34.1 59.3 %collective-permute-start.2 = (bf16[3,3,192,384]{3,2,1,0:T(8,128)(2,1)S(1)}, bf16[3,3,192,384]{3,2,1,0:T(8,128)(2,1)S(1)}, u32[]{:S(2)}, u32[]{:S(2)}) collective-permute-start(bf16[3,3,192,384]{3,2,1,0:T(8,128)(2,1)S(1)} %copy-done), channel_id=1, source_target_pairs={{0,4},{4,8},{8,12},{12,0},{1,5},{5,9},{9,13},{13,1},{2,6},{6,10},{... | collective-permute-start | bytes 3981320 | tf_op jit(solution)/shard_map/ppermute | solution.py:106
  45.0 48.4 %copy-start.5 = (bf16[592,4,64]{2,1,0:T(4,128)(2,1)S(1)}, bf16[592,4,64]{2,1,0:T(4,128)(2,1)}, u32[]{:S(2)}) copy-start(bf16[592,4,64]{2,1,0:T(4,128)(2,1)} %reshape.93) | copy-start | bytes 909316
  93.4 33.0 %collective-permute-start.3 = (bf16[3,3,192,384]{3,2,1,0:T(8,128)(2,1)S(1)}, bf16[3,3,192,384]{3,2,1,0:T(8,128)(2,1)}, u32[]{:S(2)}, u32[]{:S(2)}) collective-permute-start(bf16[3,3,192,384]{3,2,1,0:T(8,128)(2,1)S(1)} %collective-permute-done.2), channel_id=1, source_target_pairs={{0,4},{4,8},{8,12},{12,0},{1,5},{5,9},{9,13},{13,1},{2,6},{6,10},{... | collective-permute-start | bytes 3981320 | tf_op jit(solution)/shard_map/ppermute | solution.py:106
  107.6 4.4 %collective-permute-start.1 = (bf16[1,74,768]{2,1,0:T(8,128)(2,1)}, bf16[1,74,768]{2,1,0:T(8,128)(2,1)S(1)}, u32[]{:S(2)}, u32[]{:S(2)}) collective-permute-start(bf16[1,74,768]{2,1,0:T(8,128)(2,1)} %get-tuple-element.61), channel_id=1, source_target_pairs={{1,0},{2,1},{3,2},{5,4},{6,5},{7,6},{9,8},{10,9},{11,10},{13,12},{... | collective-permute-start | bytes 341000 | tf_op jit(solution)/shard_map/ppermute | solution.py:22
  108.9 4.0 %collective-permute-start = (bf16[1,74,768]{2,1,0:T(8,128)(2,1)S(1)}, bf16[1,74,768]{2,1,0:T(8,128)(2,1)S(1)}, u32[]{:S(2)}, u32[]{:S(2)}) collective-permute-start(bf16[1,74,768]{2,1,0:T(8,128)(2,1)S(1)} %get-tuple-element.60), channel_id=1, source_target_pairs={{0,1},{1,2},{2,3},{4,5},{5,6},{6,7},{8,9},{9,10},{10,11},{12,13},{... | collective-permute-start | bytes 341000 | tf_op jit(solution)/shard_map/ppermute | solution.py:20
  112.9 13.5 %copy-start.6 = (bf16[1,74,768]{2,1,0:T(8,128)(2,1)}, bf16[1,74,768]{2,1,0:T(8,128)(2,1)S(1)}, u32[]{:S(2)}) copy-start(bf16[1,74,768]{2,1,0:T(8,128)(2,1)S(1)} %collective-permute-done) | copy-start | bytes 340996
  126.4 32.3 %collective-permute-start.4 = (bf16[3,3,192,384]{3,2,1,0:T(8,128)(2,1)}, bf16[3,3,192,384]{3,2,1,0:T(8,128)(2,1)}, u32[]{:S(2)}, u32[]{:S(2)}) collective-permute-start(bf16[3,3,192,384]{3,2,1,0:T(8,128)(2,1)} %collective-permute-done.3), channel_id=1, source_target_pairs={{0,4},{4,8},{8,12},{12,0},{1,5},{5,9},{9,13},{13,1},{2,6},{6,10},{... | collective-permute-start | bytes 3981320 | tf_op jit(solution)/shard_map/ppermute | solution.py:106
  141.1 4.9 %copy-start.3 = (bf16[148,768]{1,0:T(8,128)(2,1)S(1)}, bf16[148,768]{1,0:T(8,128)(2,1)}, u32[]{:S(2)}) copy-start(bf16[148,768]{1,0:T(8,128)(2,1)} %reshape.87) | copy-start | bytes 681988
  141.1 4.9 %copy-start.4 = (bf16[148,768]{1,0:T(8,128)(2,1)S(1)}, bf16[148,768]{1,0:T(8,128)(2,1)}, u32[]{:S(2)}) copy-start(bf16[148,768]{1,0:T(8,128)(2,1)} %reshape.88) | copy-start | bytes 681988
Sparse Core Ops, SparseCore 0:
  25.1 64.0 all-gather.1
